TPU v7x, 32 devices: a whole 2x2x4 slice. The times are simulated.
32 devices in a mesh: seq: 8 (over z, core), head: 4 (over y, x).
Axes of the slice: x: 2, y: 2, z: 4, core: 2. Of those that a mesh axis runs over, the one named last changes fastest.
Arguments:
- queries: bfloat16 [1024, 128, 576], P('seq', 'head'), may hold values from -24 to 24
- latent_kv: bfloat16 [1024, 576], P('seq'), may hold values from -4.5 to 4.5
- grad_out: bfloat16 [1024, 128, 512], P('seq', 'head'), may hold values from -6 to 6
- doc_start: int32 [1024], P('seq'), may hold values from 0 to 1023, as said below
Outputs:
- grad_queries: bfloat16 [1024, 128, 576], P('seq', 'head')
- grad_latent: float32 [1024, 576], P('seq')
Inputs may be any that keep to these rules, and one draw needn't show every extreme that they name: doc_start[p] is the first position of the document holding position p: it never falls along the sequence, doc_start[p] <= p, doc_start[0] = 0, every document holds at most 385 positions, and one document holds exactly 385.
All inputs are finite; a program needn't handle non-finite values.
Results may differ from a plain program's by a relative error of at most 0.0048.
Values may be sent and summed in bfloat16 or wider, within the bound.
A program may use at most 128 MiB of HBM per device.

v0:
```python
import math
from functools import partial

import jax
import jax.numpy as jnp
from jax import lax
from jax.experimental import pallas as pl
from jax.experimental.pallas import tpu as pltpu
from jax.sharding import PartitionSpec as P

LAT = 512
REACH = 4


softmax_scale = 192.0 ** (-0.5)
lowest = -1e30
contract_last = (((1,), (1,)), ((), ()))
contract_first = (((0,), (0,)), ((), ()))


def passed_along(block, axis, distance):
    devices = range(lax.axis_size(axis))
    route = [(i - distance, i) for i in devices if i - distance in devices]
    return lax.ppermute(block, axis, route)


def product_tiles(query_rows, grad_rows, kv_block, unused):
    scores = (
        lax.dot_general(query_rows, kv_block, contract_last, preferred_element_type=jnp.float32)
        * softmax_scale
    )
    grad_probs = lax.dot_general(
        grad_rows, kv_block[:, :LAT], contract_last, preferred_element_type=jnp.float32
    )
    return (scores, grad_probs)


def empty_tiles(query_count, key_count, unused):
    blank = jnp.zeros((query_count, key_count), jnp.float32)
    return (blank, blank)


def grads_update(
    query_rows, grad_rows, kv_block, scores, grad_probs, visible, log_total, row_delta, unused
):
    weights = jnp.where(visible, jnp.exp(scores - log_total[:, None]), 0.0)
    grad_bf = (weights * (grad_probs - row_delta[:, None])).astype(jnp.bfloat16)
    prob_bf = weights.astype(jnp.bfloat16)
    query_part = jnp.dot(grad_bf, kv_block, preferred_element_type=jnp.float32)
    from_scores = (
        lax.dot_general(grad_bf, query_rows, contract_first, preferred_element_type=jnp.float32)
        * softmax_scale
    )
    from_values = lax.dot_general(
        prob_bf, grad_rows, contract_first, preferred_element_type=jnp.float32
    )
    term = jnp.concatenate([from_scores[:, :LAT] + from_values, from_scores[:, LAT:]], axis=1)
    return (query_part, term)


def no_grads(query_count, tokens, row_width, unused):
    return (
        jnp.zeros((query_count, row_width), jnp.float32),
        jnp.zeros((tokens, row_width), jnp.float32),
    )


def per_device(queries, latent_kv, grad_out, doc_start):
    tokens, head_local, row_width = queries.shape
    query_count = tokens * head_local
    first_pos = lax.axis_index("seq") * tokens
    query_rows = queries.reshape(query_count, row_width)
    grad_rows = grad_out.reshape(query_count, LAT)
    row_pos = jnp.repeat(first_pos + jnp.arange(tokens, dtype=jnp.int32), head_local)
    row_first = jnp.repeat(doc_start, head_local)
    low_first = jnp.min(doc_start)
    windows = [latent_kv]
    for distance in range(1, REACH):
        windows.append(passed_along(latent_kv, "seq", distance))
    key_starts = [first_pos - distance * tokens for distance in range(REACH)]
    wanted = [start + tokens > low_first for start in key_starts]
    blank = jnp.zeros((query_count,), jnp.float32)
    row_top = jnp.full((query_count,), lowest, jnp.float32)
    total_exp = blank
    weighted = blank
    kept = []
    for distance in range(REACH):
        scores, grad_probs = lax.cond(
            wanted[distance],
            partial(product_tiles, query_rows, grad_rows, windows[distance]),
            partial(empty_tiles, query_count, tokens),
            0,
        )
        key_pos = key_starts[distance] + jnp.arange(tokens, dtype=jnp.int32)
        visible = (key_pos[None, :] <= row_pos[:, None]) & (key_pos[None, :] >= row_first[:, None])
        new_top = jnp.maximum(row_top, jnp.max(jnp.where(visible, scores, lowest), axis=1))
        rescale = jnp.exp(row_top - new_top)
        weights = jnp.where(visible, jnp.exp(scores - new_top[:, None]), 0.0)
        total_exp = total_exp * rescale + jnp.sum(weights, axis=1)
        weighted = weighted * rescale + jnp.sum(weights * grad_probs, axis=1)
        row_top = new_top
        kept.append((scores, grad_probs, visible))
    log_total = row_top + jnp.log(total_exp)
    row_delta = weighted / total_exp
    query_grad = jnp.zeros((query_count, row_width), jnp.float32)
    terms = []
    for distance in range(REACH):
        scores, grad_probs, visible = kept[distance]
        compute = partial(
            grads_update,
            query_rows,
            grad_rows,
            windows[distance],
            scores,
            grad_probs,
            visible,
            log_total,
            row_delta,
        )
        query_part, term = lax.cond(
            wanted[distance], compute, partial(no_grads, query_count, tokens, row_width), 0
        )
        query_grad = query_grad + query_part
        terms.append(term)
    own_rows = terms[0]
    for distance in range(1, REACH):
        own_rows = own_rows + passed_along(
            terms[distance].astype(jnp.bfloat16), "seq", -distance
        ).astype(jnp.float32)
    grad_latent = lax.psum(own_rows, "head")
    grad_queries = (
        (softmax_scale * query_grad).astype(jnp.bfloat16).reshape(tokens, head_local, row_width)
    )
    return (grad_queries, grad_latent)


TILE_HEADS = 4
MESH = pl.DeviceIdType.MESH


def fused_kernel(
    n_seq, n_head, head_local, tokens,
    q_hbm, g_hbm, kv_ref, first_ref,
    dq_hbm, out_ref,
    q, g, dq, ds, pb, win, win_t, bias, parts, *rest,
):
    cuts = parts
    n_cut = len(cuts)
    take = iter(rest)
    own = [next(take) for _ in range(n_cut)]
    t_send = [next(take) for _ in range(n_cut)]
    t_recv = [next(take) for _ in range(n_cut)]
    r_send = [next(take) for _ in range(n_cut)]
    r_recv = [next(take) for _ in range(n_cut)]
    r_own = [next(take) for _ in range(n_cut)]
    f_send = [next(take) for _ in range(n_cut)]
    f_recv = [next(take) for _ in range(n_cut)]
    (load_sem, q_sem, store_sem, g1s, g1r, g2s, g2r, r1s, r1r, r2s, r2r, r3s, r3r) = take

    s = lax.axis_index("seq")
    h = lax.axis_index("head")
    width = kv_ref.shape[1]
    quarter = tokens // n_head
    tile_rows = TILE_HEADS * tokens
    n_tile = head_local // TILE_HEADS
    margin = (REACH - 1) * tokens
    window = REACH * tokens
    peers = range(1, n_head)
    reach = range(1, REACH)

    def peer(k):
        return lax.rem(h + k, n_head)

    def load_q(i):
        lanes = pl.ds(pl.multiple_of(i * tokens, tokens), tokens)
        return pltpu.make_async_copy(q_hbm.at[i], q.at[:, lanes], q_sem.at[i])

    loads = [
        pltpu.make_async_copy(g_hbm, g, load_sem.at[0]),
        pltpu.make_async_copy(kv_ref, win.at[pl.ds(margin, tokens)], load_sem.at[1]),
    ]
    for copy in loads:
        copy.start()

    @pl.loop(0, head_local)
    def _(i):
        load_q(i).start()

    barrier = pltpu.get_barrier_semaphore()
    for k in peers:
        pl.semaphore_signal(barrier, inc=1, device_id=(s, peer(k)), device_id_type=MESH)
    for d in reach:
        @pl.when(s >= d)
        def _():
            pl.semaphore_signal(barrier, inc=1, device_id=(s - d, h), device_id_type=MESH)

        @pl.when(s + d < n_seq)
        def _():
            pl.semaphore_signal(barrier, inc=1, device_id=(s + d, h), device_id_type=MESH)

    before = jnp.minimum(s, REACH - 1)
    after = jnp.minimum(n_seq - 1 - s, REACH - 1)
    pl.semaphore_wait(barrier, n_head - 1 + before + after)

    share = pl.multiple_of(h * quarter, quarter)

    def along(d):
        return pltpu.make_async_remote_copy(
            src_ref=kv_ref.at[pl.ds(share, quarter)],
            dst_ref=win.at[pl.ds((REACH - 1 - d) * tokens + share, quarter)],
            send_sem=g1s.at[d - 1], recv_sem=g1r.at[d - 1],
            device_id=(s + d, h), device_id_type=MESH,
        )

    def across(d, k):
        rows = pl.ds((REACH - 1 - d) * tokens + share, quarter)
        return pltpu.make_async_remote_copy(
            src_ref=win.at[rows], dst_ref=win.at[rows],
            send_sem=g2s.at[d - 1, k - 1], recv_sem=g2r.at[d - 1, k - 1],
            device_id=(s, peer(k)), device_id_type=MESH,
        )

    for d in reach:
        @pl.when(s + d < n_seq)
        def _():
            along(d).start()

        @pl.when(s < d)
        def _():
            win[pl.ds((REACH - 1 - d) * tokens, tokens), :] = jnp.zeros((tokens, width), win.dtype)

    for d in reach:
        @pl.when(s >= d)
        def _():
            along(d).wait_recv()
            for k in peers:
                across(d, k).start()

    base = s * tokens - margin
    key = lax.broadcasted_iota(jnp.int32, (window, tokens), 0)
    last = margin + lax.broadcasted_iota(jnp.int32, (window, tokens), 1)
    bias[...] = jnp.where((key <= last) & (key >= first_ref[...] - base), 0.0, lowest)
    for copy in loads:
        copy.wait()

    @pl.loop(0, head_local)
    def _(i):
        load_q(i).wait()

    for d in reach:
        @pl.when(s >= d)
        def _():
            for k in peers:
                across(d, k).wait()

        @pl.when(s + d < n_seq)
        def _():
            along(d).wait_send()

    win_t[...] = win[...].T
    rate = softmax_scale * math.log2(math.e)

    def tile_products(i):
        rows = pl.ds(pl.multiple_of(i * tile_rows, tile_rows), tile_rows)
        scores = jnp.dot(win[...], q[:, rows], preferred_element_type=jnp.float32)
        grad_probs = lax.dot_general(
            win[:, :LAT], g[rows, :], contract_last, preferred_element_type=jnp.float32
        )
        return scores, grad_probs

    def tile_softmax(i, scores, grad_probs):
        for j in range(TILE_HEADS):
            part = slice(j * tokens, (j + 1) * tokens)
            lanes = pl.ds(pl.multiple_of(i * tile_rows + j * tokens, tokens), tokens)
            shown = scores[:, part] + bias[...]
            grads = grad_probs[:, part]
            top = jnp.max(shown, axis=0, keepdims=True)
            weights = jnp.exp2((shown - top) * rate)
            inverse = 1.0 / jnp.sum(weights, axis=0, keepdims=True)
            delta = jnp.sum(weights * grads, axis=0, keepdims=True) * inverse
            probs = weights * inverse
            ds[:, lanes] = (probs * (grads - delta)).astype(ds.dtype)
            pb[:, lanes] = probs.astype(pb.dtype)

    def softmax_pair(j, carry):
        first, second = tile_products(2 * j), tile_products(2 * j + 1)
        tile_softmax(2 * j, *first)
        tile_softmax(2 * j + 1, *second)
        return carry

    lax.fori_loop(0, n_tile // 2, softmax_pair, 0)

    def head_copy(c, k):
        return pltpu.make_async_remote_copy(
            src_ref=t_send[c].at[peer(k)], dst_ref=t_recv[c].at[k - 1],
            send_sem=r1s.at[c, k - 1], recv_sem=r1r.at[c, k - 1],
            device_id=(s, peer(k)), device_id_type=MESH,
        )

    def seq_copy(c, d):
        return pltpu.make_async_remote_copy(
            src_ref=r_send[c].at[d - 1], dst_ref=r_recv[c].at[d - 1],
            send_sem=r2s.at[c, d - 1], recv_sem=r2r.at[c, d - 1],
            device_id=(s - d, h), device_id_type=MESH,
        )

    def last_copy(c, k):
        return pltpu.make_async_remote_copy(
            src_ref=f_send[c], dst_ref=f_recv[c].at[k - 1],
            send_sem=r3s.at[c, k - 1], recv_sem=r3r.at[c, k - 1],
            device_id=(s, peer(k)), device_id_type=MESH,
        )

    def latent_part(c):
        low, high = cuts[c]
        split = min(high, LAT)
        term = lax.dot_general(
            ds[...], q[low:high, :], contract_last, preferred_element_type=jnp.float32
        ) * softmax_scale
        value = jnp.dot(pb[...], g[:, low:split], preferred_element_type=jnp.float32)
        if split < high:
            own[c][:, : split - low] = term[:, : split - low] + value
            own[c][:, split - low :] = term[:, split - low :]
        else:
            own[c][...] = term + value
        for j in range(n_head):
            for b in range(REACH):
                t_send[c][j, b * quarter : (b + 1) * quarter, :] = own[c][
                    b * tokens + j * quarter : b * tokens + (j + 1) * quarter, :
                ].astype(jnp.bfloat16)
        for k in peers:
            head_copy(c, k).start()

    def head_sum(c):
        for k in peers:
            head_copy(c, k).wait()
        for b in range(REACH):
            total = own[c][pl.ds(b * tokens + share, quarter), :]
            for k in peers:
                total = total + t_recv[c][k - 1, b * quarter : (b + 1) * quarter, :].astype(jnp.float32)
            d = REACH - 1 - b
            if d == 0:
                r_own[c][...] = total
            else:
                r_send[c][d - 1] = total.astype(jnp.bfloat16)

                @pl.when(s >= d)
                def _():
                    seq_copy(c, d).start()

    def seq_sum(c):
        for d in reach:
            @pl.when(s + d < n_seq)
            def _():
                seq_copy(c, d).wait_recv()
                r_own[c][...] = r_own[c][...] + r_recv[c][d - 1].astype(jnp.float32)

            @pl.when(s >= d)
            def _():
                seq_copy(c, d).wait_send()

        f_send[c][...] = r_own[c][...]
        for k in peers:
            last_copy(c, k).start()
        low, high = cuts[c]
        out_ref[pl.ds(share, quarter), low:high] = r_own[c][...]

    def collect(c):
        low, high = cuts[c]
        for k in peers:
            last_copy(c, k).wait()
            source = lax.rem(h + n_head - k, n_head)
            out_ref[pl.ds(pl.multiple_of(source * quarter, quarter), quarter), low:high] = f_recv[c][k - 1]

    def query_tile(i):
        rows = pl.ds(pl.multiple_of(i * tile_rows, tile_rows), tile_rows)
        part = jnp.dot(win_t[...], ds[:, rows], preferred_element_type=jnp.float32)
        part = (part * softmax_scale).astype(dq.dtype)
        for j in range(TILE_HEADS):
            dq[i * TILE_HEADS + j] = part[:, j * tokens : (j + 1) * tokens]

    def query_store(i):
        heads = pl.ds(i * TILE_HEADS, TILE_HEADS)
        return pltpu.make_async_copy(dq.at[heads], dq_hbm.at[heads], store_sem.at[i])

    def query_tiles(low, high):
        def one(i, carry):
            query_tile(i)
            query_store(i).start()
            return carry

        lax.fori_loop(low, high, one, 0)

    for c in range(n_cut):
        latent_part(c)
    query_tiles(0, n_tile // 4)
    head_sum(0)
    query_tiles(n_tile // 4, n_tile - n_tile // 4)
    for c in range(1, n_cut):
        head_sum(c)
    seq_sum(0)
    query_tiles(n_tile - n_tile // 4, n_tile)
    for c in range(1, n_cut):
        seq_sum(c)
    for c in range(n_cut):
        collect(c)
    for i in range(n_tile):
        query_store(i).wait()


def fused_per_device(n_seq, n_head, queries, latent_kv, grad_out, doc_start):
    tokens, head_local, width = queries.shape
    rows = tokens * head_local
    quarter = tokens // n_head
    cuts = ((LAT // 2, width), (0, LAT // 2))
    sizes = [high - low for low, high in cuts]
    bf, f32 = jnp.bfloat16, jnp.float32
    first = doc_start.reshape(1, tokens)
    window = REACH * tokens
    scratch = [
        pltpu.VMEM((width, rows), bf),
        pltpu.VMEM((rows, LAT), bf),
        pltpu.VMEM((head_local, width, tokens), bf),
        pltpu.VMEM((window, rows), bf),
        pltpu.VMEM((window, rows), bf),
        pltpu.VMEM((window, width), bf),
        pltpu.VMEM((width, window), bf),
        pltpu.VMEM((window, tokens), f32),
    ]
    scratch += [pltpu.VMEM((window, n), f32) for n in sizes]
    scratch += [pltpu.VMEM((n_head, REACH * quarter, n), bf) for n in sizes]
    scratch += [pltpu.VMEM((n_head - 1, REACH * quarter, n), bf) for n in sizes]
    scratch += [pltpu.VMEM((REACH - 1, quarter, n), bf) for n in sizes]
    scratch += [pltpu.VMEM((REACH - 1, quarter, n), bf) for n in sizes]
    scratch += [pltpu.VMEM((quarter, n), f32) for n in sizes]
    scratch += [pltpu.VMEM((quarter, n), f32) for n in sizes]
    scratch += [pltpu.VMEM((n_head - 1, quarter, n), f32) for n in sizes]
    dma = pltpu.SemaphoreType.DMA
    n_cut = len(cuts)
    scratch += [dma((2,)), dma((head_local,)), dma((head_local // TILE_HEADS,))]
    scratch += [dma((REACH - 1,)), dma((REACH - 1,))]
    scratch += [dma((REACH - 1, n_head - 1)), dma((REACH - 1, n_head - 1))]
    scratch += [dma((n_cut, n_head - 1)), dma((n_cut, n_head - 1))]
    scratch += [dma((n_cut, REACH - 1)), dma((n_cut, REACH - 1))]
    scratch += [dma((n_cut, n_head - 1)), dma((n_cut, n_head - 1))]

    def body(*refs):
        fused_kernel(n_seq, n_head, head_local, tokens, *refs[:14], cuts, *refs[14:])

    vmem = pl.BlockSpec(memory_space=pltpu.VMEM)
    anywhere = pl.BlockSpec(memory_space=pl.ANY)
    grad_rows, grad_latent = pl.pallas_call(
        body,
        out_shape=(
            jax.ShapeDtypeStruct((head_local, width, tokens), bf),
            jax.ShapeDtypeStruct((tokens, width), f32),
        ),
        in_specs=[anywhere, anywhere, vmem, vmem],
        out_specs=(anywhere, vmem),
        scratch_shapes=scratch,
        compiler_params=pltpu.CompilerParams(
            collective_id=0, has_side_effects=True, vmem_limit_bytes=60 * 1024 * 1024
        ),
    )(
        queries.transpose(1, 2, 0),
        grad_out.transpose(1, 0, 2).reshape(rows, LAT),
        latent_kv,
        first,
    )
    return grad_rows.transpose(2, 0, 1), grad_latent


def solution(mesh):
    in_specs = (P("seq", "head", None), P("seq", None), P("seq", "head", None), P("seq"))
    out_specs = (P("seq", "head", None), P("seq", None))
    n_seq, n_head = mesh.shape["seq"], mesh.shape["head"]

    def routed(queries, latent_kv, grad_out, doc_start):
        tokens, head_local, _ = queries.shape
        fits = (
            n_head > 1
            and tokens % 128 == 0
            and tokens % (16 * n_head) == 0
            and head_local % (2 * TILE_HEADS) == 0
            and n_seq >= REACH
        )
        run = partial(fused_per_device, n_seq, n_head) if fits else per_device
        return run(queries, latent_kv, grad_out, doc_start)

    return jax.shard_map(
        routed, mesh=mesh, in_specs=in_specs, out_specs=out_specs, check_vma=False
    )
```

profile of v0, /device:TPU:0, one launch (start us, length us, event | category | flops | bytes accessed | tf_op | source)
XLA Modules:
  0.0 61.6 jit_solution(16568305346612282313)
XLA Ops:
  0.6 1.7 %copy.7.refs_2_ = bf16[128,576]{1,0:T(8,128)(2,1)} copy(bf16[128,576]{0,1:T(8,128)(2,1)} %param.5) | data formatting | bytes 294912 | tf_op args[1]
  2.3 6.5 %copy.6 = bf16[32,128,512]{2,1,0:T(8,128)(2,1)} copy(bf16[32,128,512]{2,0,1:T(8,128)(2,1)} %bitcast.8) | data formatting | bytes 8388608 | tf_op jit(solution)/shard_map/transpose | solution.py:466
  8.9 46.0 %shard_map.59 = (bf16[32,576,128]{2,1,0:T(8,128)(2,1)}, f32[128,576]{1,0:T(8,128)}) custom-call(bf16[32,576,128]{2,1,0:T(8,128)(2,1)} %bitcast.6, bf16[4096,512]{1,0:T(8,128)(2,1)} %bitcast.5, bf16[128,576]{1,0:T(8,128)(2,1)} %copy.7.refs_2_, s32[1,128]{1,0:T(1,128)} %bitcast.9), custom_call_target="tpu_custom_call" | custom-call | tf_op jit(solution)/shard_map/pallas_call | solution.py:452
  54.9 1.8 %copy.8 = f32[128,576]{0,1:T(8,128)} copy(f32[128,576]{1,0:T(8,128)} %get-tuple-element.7) | data formatting | bytes 589824
  56.7 4.8 %copy.10 = bf16[128,32,576]{0,2,1:T(8,128)(2,1)} copy(bf16[128,32,576]{0,2,1:T(8,128)(2,1)} %bitcast.7) | data formatting | bytes 9437184
where the time goes:
time: 61.8 us; the launch traced here: 61.6 us
  Pallas kernels  46 us (74%)
  local copies, waits for them, and re-layouts  14.9 us (24%)
  between operations  0.64 us (1%)
    pallas_call x1, Pallas kernels, fused_per_device(): pl.pallas_call(body, out_shape=(jax.ShapeDtypeStruct((head_local, width,...  46 us
    unnamed x3, local copies, waits for them, and re-layouts  8.39 us
    transpose x1, local copies, waits for them, and re-layouts, fused_per_device(): grad_out.transpose(1, 0, 2).reshape(rows, LAT)  6.54 us

commit v1 on v0

--- a/solution.py
+++ b/solution.py
@@ -140,9 +140,9 @@
 
 def fused_kernel(
     n_seq, n_head, head_local, tokens,
-    q_hbm, g_hbm, kv_ref, first_ref,
+    q_hbm, g_hbm, kv_t_ref, first_ref,
     dq_hbm, out_ref,
-    q, g, dq, ds, pb, win, win_t, bias, parts, *rest,
+    q, g_in, g, out_rows, dq, ds, pb, win, win_t, bias, parts, *rest,
 ):
     cuts = parts
     n_cut = len(cuts)
@@ -159,7 +159,7 @@
 
     s = lax.axis_index("seq")
     h = lax.axis_index("head")
-    width = kv_ref.shape[1]
+    width = kv_t_ref.shape[0]
     quarter = tokens // n_head
     tile_rows = TILE_HEADS * tokens
     n_tile = head_local // TILE_HEADS
@@ -175,17 +175,19 @@
         lanes = pl.ds(pl.multiple_of(i * tokens, tokens), tokens)
         return pltpu.make_async_copy(q_hbm.at[i], q.at[:, lanes], q_sem.at[i])
 
-    loads = [
-        pltpu.make_async_copy(g_hbm, g, load_sem.at[0]),
-        pltpu.make_async_copy(kv_ref, win.at[pl.ds(margin, tokens)], load_sem.at[1]),
-    ]
-    for copy in loads:
-        copy.start()
+    def load_g(i):
+        toks = pl.ds(i * half, half)
+        return pltpu.make_async_copy(g_hbm.at[toks], g_in.at[toks], load_sem.at[i])
+
+    half = tokens // 2
+    for i in range(2):
+        load_g(i).start()
 
     @pl.loop(0, head_local)
     def _(i):
         load_q(i).start()
 
+    win[margin:, :] = kv_t_ref[...].T
     barrier = pltpu.get_barrier_semaphore()
     for k in peers:
         pl.semaphore_signal(barrier, inc=1, device_id=(s, peer(k)), device_id_type=MESH)
@@ -206,7 +208,7 @@
 
     def along(d):
         return pltpu.make_async_remote_copy(
-            src_ref=kv_ref.at[pl.ds(share, quarter)],
+            src_ref=win.at[pl.ds(margin + share, quarter)],
             dst_ref=win.at[pl.ds((REACH - 1 - d) * tokens + share, quarter)],
             send_sem=g1s.at[d - 1], recv_sem=g1r.at[d - 1],
             device_id=(s + d, h), device_id_type=MESH,
@@ -229,19 +231,28 @@
         def _():
             win[pl.ds((REACH - 1 - d) * tokens, tokens), :] = jnp.zeros((tokens, width), win.dtype)
 
-    for d in reach:
-        @pl.when(s >= d)
-        def _():
-            along(d).wait_recv()
-            for k in peers:
-                across(d, k).start()
-
     base = s * tokens - margin
     key = lax.broadcasted_iota(jnp.int32, (window, tokens), 0)
     last = margin + lax.broadcasted_iota(jnp.int32, (window, tokens), 1)
     bias[...] = jnp.where((key <= last) & (key >= first_ref[...] - base), 0.0, lowest)
-    for copy in loads:
-        copy.wait()
+    def by_head(i):
+        load_g(i).wait()
+
+        @pl.loop(0, half // 16)
+        def _(j):
+            toks = pl.ds(pl.multiple_of(i * half + j * 16, 16), 16)
+            block = g_in[toks].astype(jnp.float32)
+            g[:, toks, :] = jnp.swapaxes(block, 0, 1).astype(g.dtype)
+
+    by_head(0)
+    for d in reach:
+        @pl.when(s >= d)
+        def _():
+            along(d).wait_recv()
+            for k in peers:
+                across(d, k).start()
+
+    by_head(1)
 
     @pl.loop(0, head_local)
     def _(i):
@@ -264,7 +275,7 @@
         rows = pl.ds(pl.multiple_of(i * tile_rows, tile_rows), tile_rows)
         scores = jnp.dot(win[...], q[:, rows], preferred_element_type=jnp.float32)
         grad_probs = lax.dot_general(
-            win[:, :LAT], g[rows, :], contract_last, preferred_element_type=jnp.float32
+            win[:, :LAT], g[pl.ds(i * TILE_HEADS, TILE_HEADS)].reshape(tile_rows, LAT), contract_last, preferred_element_type=jnp.float32
         )
         return scores, grad_probs
 
@@ -317,7 +328,8 @@
         term = lax.dot_general(
             ds[...], q[low:high, :], contract_last, preferred_element_type=jnp.float32
         ) * softmax_scale
-        value = jnp.dot(pb[...], g[:, low:split], preferred_element_type=jnp.float32)
+        grads = g[:, :, low:split].reshape(head_local * tokens, split - low)
+        value = jnp.dot(pb[...], grads, preferred_element_type=jnp.float32)
         if split < high:
             own[c][:, : split - low] = term[:, : split - low] + value
             own[c][:, split - low :] = term[:, split - low :]
@@ -363,14 +375,14 @@
         for k in peers:
             last_copy(c, k).start()
         low, high = cuts[c]
-        out_ref[pl.ds(share, quarter), low:high] = r_own[c][...]
+        out_rows[pl.ds(share, quarter), low:high] = r_own[c][...]
 
     def collect(c):
         low, high = cuts[c]
         for k in peers:
             last_copy(c, k).wait()
             source = lax.rem(h + n_head - k, n_head)
-            out_ref[pl.ds(pl.multiple_of(source * quarter, quarter), quarter), low:high] = f_recv[c][k - 1]
+            out_rows[pl.ds(pl.multiple_of(source * quarter, quarter), quarter), low:high] = f_recv[c][k - 1]
 
     def query_tile(i):
         rows = pl.ds(pl.multiple_of(i * tile_rows, tile_rows), tile_rows)
@@ -404,6 +416,7 @@
         seq_sum(c)
     for c in range(n_cut):
         collect(c)
+    out_ref[...] = out_rows[...].T
     for i in range(n_tile):
         query_store(i).wait()
 
@@ -419,7 +432,9 @@
     window = REACH * tokens
     scratch = [
         pltpu.VMEM((width, rows), bf),
-        pltpu.VMEM((rows, LAT), bf),
+        pltpu.VMEM((tokens, head_local, LAT), bf),
+        pltpu.VMEM((head_local, tokens, LAT), bf),
+        pltpu.VMEM((tokens, width), f32),
         pltpu.VMEM((head_local, width, tokens), bf),
         pltpu.VMEM((window, rows), bf),
         pltpu.VMEM((window, rows), bf),
@@ -445,7 +460,7 @@
     scratch += [dma((n_cut, n_head - 1)), dma((n_cut, n_head - 1))]
 
     def body(*refs):
-        fused_kernel(n_seq, n_head, head_local, tokens, *refs[:14], cuts, *refs[14:])
+        fused_kernel(n_seq, n_head, head_local, tokens, *refs[:16], cuts, *refs[16:])
 
     vmem = pl.BlockSpec(memory_space=pltpu.VMEM)
     anywhere = pl.BlockSpec(memory_space=pl.ANY)
@@ -453,7 +468,7 @@
         body,
         out_shape=(
             jax.ShapeDtypeStruct((head_local, width, tokens), bf),
-            jax.ShapeDtypeStruct((tokens, width), f32),
+            jax.ShapeDtypeStruct((width, tokens), f32),
         ),
         in_specs=[anywhere, anywhere, vmem, vmem],
         out_specs=(anywhere, vmem),
@@ -463,11 +478,11 @@
         ),
     )(
         queries.transpose(1, 2, 0),
-        grad_out.transpose(1, 0, 2).reshape(rows, LAT),
-        latent_kv,
+        grad_out,
+        latent_kv.T,
         first,
     )
-    return grad_rows.transpose(2, 0, 1), grad_latent
+    return grad_rows.transpose(2, 0, 1), grad_latent.T
 
 
 def solution(mesh):

time: 61.8 us -> 52.3 us (0.85)
  local copies, waits for them, and re-layouts: 14.9 us -> 5.61 us
    transpose x1 -> x0, local copies, waits for them, and re-layouts: 6.54 us -> none  [fused_per_device(): grad_out.transpose(1, 0, 2).reshape(rows, LAT)]
    unnamed x3 -> x4, local copies, waits for them, and re-layouts: 8.39 us -> 5.61 us
where the time goes in v1:
time: 52.3 us; the launch traced here: 52.2 us
  Pallas kernels  45.9 us (88%)
  local copies, waits for them, and re-layouts  5.61 us (11%)
  between operations  0.65 us (1%)
    pallas_call x1, Pallas kernels, fused_per_device(): pl.pallas_call(body, out_shape=(jax.ShapeDtypeStruct((head_local, width,...  45.9 us
    unnamed x4, local copies, waits for them, and re-layouts  5.61 us

profile of v1, /device:TPU:0, one launch (start us, length us, event | category | flops | bytes accessed | tf_op | source)
XLA Modules:
  0.0 52.2 jit_solution(1856603661863196188)
XLA Ops:
  0.6 45.9 %shard_map.59 = (bf16[32,576,128]{2,1,0:T(8,128)(2,1)}, f32[576,128]{1,0:T(8,128)}) custom-call(bf16[32,576,128]{2,1,0:T(8,128)(2,1)} %bitcast.5, bf16[128,32,512]{2,1,0:T(8,128)(2,1)} %refs_1_.1, bf16[576,128]{1,0:T(8,128)(2,1)} %bitcast.8, s32[1,128]{1,0:T(1,128)} %bitcast.9), custom_call_target="tpu_custom_call" | custom-call | tf_op jit(solution)/shard_map/pallas_call | solution.py:467
  46.6 0.0 copy-start
  46.6 4.9 %copy.8 = bf16[128,32,576]{0,2,1:T(8,128)(2,1)} copy(bf16[128,32,576]{0,2,1:T(8,128)(2,1)} %bitcast.6) | data formatting | bytes 9437184
  51.5 0.0 copy-done
  51.5 0.7 %copy.9 = f32[128,576]{0,1:T(8,128)} copy(f32[128,576]{0,1:T(8,128)S(1)} %bitcast.7) | data formatting | bytes 589824
Async XLA Ops:
  46.6 4.9 %copy-start = (f32[576,128]{1,0:T(8,128)S(1)}, f32[576,128]{1,0:T(8,128)}, u32[]{:S(2)}) copy-start(f32[576,128]{1,0:T(8,128)} %get-tuple-element.5) | copy-start | bytes 884740

commit v2 on v1

--- a/solution.py
+++ b/solution.py
@@ -299,7 +299,7 @@
         tile_softmax(2 * j + 1, *second)
         return carry
 
-    lax.fori_loop(0, n_tile // 2, softmax_pair, 0)
+    lax.fori_loop(0, n_tile // 2, softmax_pair, 0, unroll=2)
 
     def head_copy(c, k):
         return pltpu.make_async_remote_copy(
@@ -401,7 +401,7 @@
             query_store(i).start()
             return carry
 
-        lax.fori_loop(low, high, one, 0)
+        lax.fori_loop(low, high, one, 0, unroll=2)
 
     for c in range(n_cut):
         latent_part(c)

time: 52.3 us -> 52.7 us (level)
  no operation moved by 1% of the time
where the time goes in v2:
time: 52.7 us; the launch traced here: 52.5 us
  Pallas kernels  46.3 us (88%)
  local copies, waits for them, and re-layouts  5.61 us (11%)
  between operations  0.65 us (1%)
    pallas_call x1, Pallas kernels, fused_per_device(): pl.pallas_call(body, out_shape=(jax.ShapeDtypeStruct((head_local, width,...  46.3 us
    unnamed x4, local copies, waits for them, and re-layouts  5.61 us

profile of v2, /device:TPU:0, one launch (start us, length us, event | category | flops | bytes accessed | tf_op | source)
XLA Modules:
  0.0 52.5 jit_solution(16354302225169722802)
XLA Ops:
  0.6 46.3 %shard_map.59 = (bf16[32,576,128]{2,1,0:T(8,128)(2,1)}, f32[576,128]{1,0:T(8,128)}) custom-call(bf16[32,576,128]{2,1,0:T(8,128)(2,1)} %bitcast.5, bf16[128,32,512]{2,1,0:T(8,128)(2,1)} %refs_1_.1, bf16[576,128]{1,0:T(8,128)(2,1)} %bitcast.8, s32[1,128]{1,0:T(1,128)} %bitcast.9), custom_call_target="tpu_custom_call" | custom-call | tf_op jit(solution)/shard_map/pallas_call | solution.py:467
  46.9 0.0 copy-start
  46.9 4.9 %copy.8 = bf16[128,32,576]{0,2,1:T(8,128)(2,1)} copy(bf16[128,32,576]{0,2,1:T(8,128)(2,1)} %bitcast.6) | data formatting | bytes 9437184
  51.8 0.0 copy-done
  51.8 0.7 %copy.9 = f32[128,576]{0,1:T(8,128)} copy(f32[128,576]{0,1:T(8,128)S(1)} %bitcast.7) | data formatting | bytes 589824
Async XLA Ops:
  46.9 4.9 %copy-start = (f32[576,128]{1,0:T(8,128)S(1)}, f32[576,128]{1,0:T(8,128)}, u32[]{:S(2)}) copy-start(f32[576,128]{1,0:T(8,128)} %get-tuple-element.5) | copy-start | bytes 884740
